TPU v7x, 256 devices: a whole 4x4x8 slice. The times are simulated.
256 devices in a mesh: grp: 32 (over z, x_lo, core), patch: 8 (over y, x_hi).
Axes of the slice: x: 4 (x_hi: 2, x_lo: 2; x = x_hi * 2 + x_lo), y: 4, z: 8, core: 2. Of those that a mesh axis runs over, the one named last changes fastest.
Arguments:
- tokens: bfloat16 [98304, 1152], P(('grp', 'patch')), parts along dimension 0, may hold values from -6 to 6
- projection_weight: bfloat16 [1152, 3456], replicated, may hold values from -0.1875 to 0.1875
- shift_term: float32 [1152], replicated, may hold values from -3 to 3
- scale_term: float32 [1152], replicated, may hold values from -3 to 3
- query_gain: float32 [72], replicated, may hold values from 0.1 to 1.9
- key_gain: float32 [72], replicated, may hold values from 0.1 to 1.9
- stale_keys: bfloat16 [98304, 1152], P(('grp', 'patch')), parts along dimension 0, may hold values from -6 to 6
- stale_values: bfloat16 [98304, 1152], P(('grp', 'patch')), parts along dimension 0, may hold values from -6 to 6
- stale_output: bfloat16 [98304, 1152], P(('grp', 'patch')), parts along dimension 0, may hold values from -3 to 3
- refreshed: int32 [6144], P('grp'), parts along dimension 0, may hold values from 0 to 1, as said below
Outputs:
- attended: bfloat16 [98304, 1152], P(('grp', 'patch')), parts along dimension 0
There are 32 independent parts, one for each index of `grp`. A program takes and returns all parts, laid end to end along the dimension named above; an argument that names none is the same for every part. Nothing has to cross between parts.
Inputs may be any that keep to these rules, and one draw needn't show every extreme that they name: Exactly 64 of the 192 entries are 1; in every prompt some device has all 24 of its tiles refreshed.
All inputs are finite; a program needn't handle non-finite values.
Results may differ from a plain program's by a relative error of at most 0.0045.
Values may be sent and summed in bfloat16 or wider, within the bound.
A program may use at most 128 MiB of HBM per device.

v0:
```python
import functools
import math

import jax
import jax.numpy as jnp
from jax import lax
from jax.experimental import pallas as pl
from jax.experimental.pallas import tpu as pltpu
from jax.sharding import PartitionSpec as P

H = 16
HD = 72
TILE = 16
D = H * HD
PARTS = 8
ROWS = 384
TILES_DEV = ROWS // TILE
TILES = PARTS * TILES_DEV
REFRESHED = 64
FRESH = REFRESHED * TILE
HEADS_DEV = H // PARTS
BLOCK = 384
QBLOCK = 256
TOKEN_LOADS = 3
NORM_BLOCK = 64
MESH = pl.DeviceIdType.MESH
EPSILON = 1e-06
F32 = jnp.float32
BF16 = jnp.bfloat16

OFFSETS = ((2, 1), (2, 0), (1, 1), (3, 1), (0, 1), (1, 0), (3, 0))


def dot(a, b):
    return jnp.dot(a, b, preferred_element_type=F32)


def dot_nt(a, b):
    return lax.dot_general(a, b, (((1,), (1,)), ((), ())), preferred_element_type=F32)


def eye(n):
    rows = lax.broadcasted_iota(jnp.int32, (n, n), 0)
    columns = lax.broadcasted_iota(jnp.int32, (n, n), 1)
    return jnp.where(rows == columns, 1.0, 0.0).astype(BF16)


def kernel(
    tokens_hbm,
    weight_hbm,
    shift_ref,
    scale_ref,
    query_gain_ref,
    key_gain_ref,
    stale_keys_hbm,
    stale_values_hbm,
    stale_output_hbm,
    refreshed_ref,
    out_ref,
    tokens,
    weight,
    stale,
    hidden,
    turned,
    own_mask,
    query_send,
    kv_send,
    query_recv,
    kv_recv,
    query_rows,
    query_fresh,
    numerator,
    totals,
    attended,
    out_send,
    out_recv,
    plan_vmem,
    plan,
    load_sem,
    weight_sem,
    stale_sem,
    plan_sem,
    own_sem,
    q_send_sem,
    q_recv_sem,
    kv_send_sem,
    kv_recv_sem,
    o_send_sem,
    o_recv_sem,
):
    grp = lax.axis_index("grp")
    me = lax.axis_index("patch")
    my_y, my_x = me // 2, me % 2

    def target(k):
        dy, dx = OFFSETS[k]
        return lax.rem(my_y + dy, 4) * 2 + lax.rem(my_x + dx, 2)

    def source(k):
        dy, dx = OFFSETS[k]
        return lax.rem(my_y + 4 - dy, 4) * 2 + lax.rem(my_x + dx, 2)

    loads = []
    for part in range(TOKEN_LOADS):
        rows = pl.ds(part * (ROWS // TOKEN_LOADS), ROWS // TOKEN_LOADS)
        loads.append(pltpu.make_async_copy(tokens_hbm.at[rows], tokens.at[rows], load_sem.at[part]))
    weight_loads = []
    for part in range(3):
        columns = pl.ds(part * D, D)
        weight_loads.append(
            pltpu.make_async_copy(weight_hbm.at[:, columns], weight.at[part], weight_sem.at[part])
        )
    stale_loads = []
    for slot, ref in enumerate((stale_keys_hbm, stale_values_hbm, stale_output_hbm)):
        stale_loads.append(pltpu.make_async_copy(ref, stale.at[slot], stale_sem.at[slot]))
    for load in loads:
        load.start()
    for part in range(3):
        weight_loads[part].start()
        stale_loads[part].start()

    barrier = pltpu.get_barrier_semaphore()
    for k in range(PARTS - 1):
        pl.semaphore_signal(barrier, inc=1, device_id=(grp, target(k)), device_id_type=MESH)

    def column(gain_ref):
        same = lax.broadcasted_iota(jnp.int32, (HD, HD), 0) == lax.broadcasted_iota(
            jnp.int32, (HD, HD), 1
        )
        row = jnp.broadcast_to(gain_ref[...].reshape(1, HD), (HD, HD))
        return jnp.sum(jnp.where(same, row, 0.0), axis=1, keepdims=True)

    shift = shift_ref[...].reshape(1, D)
    scale = 1.0 + scale_ref[...].reshape(1, D)
    with jax.named_scope("norm"):
        for part in range(TOKEN_LOADS):
            loads[part].wait()
            for block in range(ROWS // TOKEN_LOADS // NORM_BLOCK):
                rows = pl.ds(part * (ROWS // TOKEN_LOADS) + block * NORM_BLOCK, NORM_BLOCK)
                values = tokens[rows, :].astype(F32)
                center = values - jnp.mean(values, axis=-1, keepdims=True)
                spread = jnp.mean(center * center, axis=-1, keepdims=True)
                normed = center * (1.0 / jnp.sqrt(spread + EPSILON))
                hidden[rows, :] = (normed * scale + shift).astype(BF16)

    def project(part):
        for block in range(D // BLOCK):
            columns = pl.ds(block * BLOCK, BLOCK)
            fresh = dot(hidden[...], weight[part, :, columns]).astype(BF16)
            if part > 0:
                mask = own_mask[...]
                mask = jnp.concatenate([mask] * (BLOCK // 128), axis=1)
                old = stale[part - 1, :, columns].astype(F32)
                fresh = jnp.where(mask > 0.5, fresh.astype(F32), old).astype(BF16)
            turned[columns, :] = fresh.T

    def head_norm(head, gain):
        values = turned[pl.ds(head * HD, HD), :].astype(F32)
        mean = jnp.sum(values * values, axis=0, keepdims=True) * (1.0 / HD)
        return (values * (1.0 / jnp.sqrt(mean + EPSILON)) * gain).astype(BF16)

    with jax.named_scope("proj_q"):
        weight_loads[0].wait()
        project(0)
    with jax.named_scope("norm_q"):
        gain = column(query_gain_ref)
        for head in range(H):
            query_send[head // HEADS_DEV, head % HEADS_DEV] = head_norm(head, gain)
    with jax.named_scope("barrier"):
        pl.semaphore_wait(barrier, PARTS - 1)

    def query_copy(k):
        return pltpu.make_async_remote_copy(
            src_ref=query_send.at[target(k)],
            dst_ref=query_recv.at[me],
            send_sem=q_send_sem.at[k],
            recv_sem=q_recv_sem.at[k],
            device_id=(grp, target(k)),
            device_id_type=MESH,
        )

    def kv_copy(head, k):
        return pltpu.make_async_remote_copy(
            src_ref=kv_send.at[head, target(k)],
            dst_ref=kv_recv.at[head, me],
            send_sem=kv_send_sem.at[head, k],
            recv_sem=kv_recv_sem.at[head, k],
            device_id=(grp, target(k)),
            device_id_type=MESH,
        )

    def out_copy(head, k):
        return pltpu.make_async_remote_copy(
            src_ref=out_send.at[head, target(k)],
            dst_ref=out_recv.at[me, head],
            send_sem=o_send_sem.at[head, k],
            recv_sem=o_recv_sem.at[head, k],
            device_id=(grp, target(k)),
            device_id_type=MESH,
        )

    own_query = pltpu.make_async_copy(query_send.at[me], query_recv.at[me], own_sem.at[0])
    own_kv = [
        pltpu.make_async_copy(kv_send.at[h, me], kv_recv.at[h, me], own_sem.at[1 + h])
        for h in range(HEADS_DEV)
    ]
    own_out = [
        pltpu.make_async_copy(out_send.at[h, me], out_recv.at[me, h], own_sem.at[3 + h])
        for h in range(HEADS_DEV)
    ]
    for k in range(PARTS - 1):
        query_copy(k).start()
    own_query.start()

    flags = refreshed_ref[...].reshape(1, TILES).astype(F32)
    tile_row = lax.broadcasted_iota(jnp.int32, (TILES, TILES), 0)
    tile_col = lax.broadcasted_iota(jnp.int32, (TILES, TILES), 1)
    flag_rows = jnp.broadcast_to(flags, (TILES, TILES))
    until = jnp.where(tile_col <= tile_row, flag_rows, 0.0).astype(BF16)
    inclusive = dot(until, jnp.ones((TILES, 128), BF16))
    slots = lax.broadcasted_iota(jnp.int32, (TILES, 128), 1).astype(F32)
    which = jnp.sum(jnp.where(inclusive <= slots, 1.0, 0.0), axis=0, keepdims=True)
    which = jnp.minimum(which, float(TILES - 1))
    before = jnp.where(tile_row < tile_col, 1.0, 0.0).astype(BF16)
    rank = dot(jnp.broadcast_to(flags, (8, TILES)).astype(BF16), before)[0:1]
    rank = jnp.minimum(rank, float(REFRESHED - 1))
    plan_vmem[0:1, 0:128] = which.astype(jnp.int32)
    plan_vmem[1:2, 0:TILES] = rank.astype(jnp.int32)
    plan_copy = pltpu.make_async_copy(plan_vmem, plan, plan_sem)
    plan_copy.start()
    row_tile = lax.broadcasted_iota(jnp.int32, (ROWS, TILES), 0) // TILE + me * TILES_DEV
    row_col = lax.broadcasted_iota(jnp.int32, (ROWS, TILES), 1)
    chosen = jnp.where(row_tile == row_col, jnp.broadcast_to(flags, (ROWS, TILES)), 0.0)
    own_mask[...] = dot(chosen.astype(BF16), jnp.ones((TILES, 128), BF16))

    with jax.named_scope("proj_k"):
        weight_loads[1].wait()
        stale_loads[0].wait()
        project(1)
    with jax.named_scope("norm_k"):
        gain = column(key_gain_ref)
        for head in range(H):
            kv_send[head % HEADS_DEV, head // HEADS_DEV, 0] = head_norm(head, gain)
    with jax.named_scope("proj_v"):
        weight_loads[2].wait()
        stale_loads[1].wait()
        project(2)
    with jax.named_scope("put_v"):
        for head in range(H):
            kv_send[head % HEADS_DEV, head // HEADS_DEV, 1] = turned[pl.ds(head * HD, HD), :]
    for h in range(HEADS_DEV):
        for k in range(PARTS - 1):
            kv_copy(h, k).start()
        own_kv[h].start()

    numerator[...] = jnp.zeros_like(numerator)
    totals[...] = jnp.zeros_like(totals)
    same = eye(ROWS)

    def turn_queries(index):
        for h in range(HEADS_DEV):
            rows = dot_nt(same, query_recv[index, h]).astype(BF16)
            query_rows[h, pl.ds(index * TILES_DEV, TILES_DEV)] = rows.reshape(TILES_DEV, TILE, HD)

    with jax.named_scope("turn_q"):
        own_query.wait()
        turn_queries(me)
        for k in range(PARTS - 1):
            query_copy(k).wait_recv()
            turn_queries(source(k))
    with jax.named_scope("keep_fresh"):
        plan_copy.wait()
        for slot in range(REFRESHED):
            tile = jnp.clip(plan[0, slot], 0, TILES - 1)
            for h in range(HEADS_DEV):
                query_fresh[h, slot] = query_rows[h, tile]
    factor = math.log2(math.e) / math.sqrt(HD)
    tiles_block = QBLOCK // TILE

    def add_block(head, index):
        keys = kv_recv[head, index, 0]
        values = kv_recv[head, index, 1]

        for block in range(FRESH // QBLOCK):
            rows = pl.ds(block * QBLOCK, QBLOCK)
            queries = query_fresh[head, pl.ds(block * tiles_block, tiles_block)]
            scores = dot(queries.reshape(QBLOCK, HD), keys)
            weights = jnp.exp2(scores * factor)
            sums = weights[:, 0:128]
            for lane in range(128, ROWS, 128):
                sums = sums + weights[:, lane : lane + 128]
            totals[head, rows, :] += sums
            numerator[head, rows, :] += dot_nt(weights.astype(BF16), values)

    def send_out(head):
        for block in range(FRESH // QBLOCK):
            rows = pl.ds(block * QBLOCK, QBLOCK)
            total = jnp.sum(totals[head, rows, :], axis=1, keepdims=True)
            result = (numerator[head, rows, :] / total).astype(BF16)
            attended[head, pl.ds(block * tiles_block, tiles_block)] = result.reshape(
                tiles_block, TILE, HD
            )

        same = eye(HD)
        for owner in range(PARTS):
            pieces = []
            for tile in range(TILES_DEV):
                item = jnp.clip(plan[1, owner * TILES_DEV + tile], 0, REFRESHED - 1)
                pieces.append(attended[head, item])
            rows = jnp.concatenate(pieces, axis=0)
            out_send[head, owner] = dot_nt(same, rows).astype(BF16)
        for k in range(PARTS - 1):
            out_copy(head, k).start()
        own_out[head].start()

    for h in range(HEADS_DEV):
        with jax.named_scope("add_own"):
            own_kv[h].wait()
            add_block(h, me)
        for k in range(PARTS - 1):
            with jax.named_scope(f"wait_kv#h={h}#k={k}"):
                kv_copy(h, k).wait_recv()
            with jax.named_scope("add"):
                add_block(h, source(k))
        with jax.named_scope("send_out"):
            send_out(h)

    with jax.named_scope("wait_out"):
        stale_loads[2].wait()
        for h in range(HEADS_DEV):
            own_out[h].wait()
            for k in range(PARTS - 1):
                out_copy(h, k).wait_recv()
    with jax.named_scope("merge"):
        for owner in range(PARTS):
            for h in range(HEADS_DEV):
                turned[pl.ds((owner * HEADS_DEV + h) * HD, HD), :] = out_recv[owner, h]
        mask = own_mask[...] > 0.5
        for block in range(D // 128):
            columns = pl.ds(block * 128, 128)
            fresh = turned[columns, :].T.astype(F32)
            out_ref[:, columns] = jnp.where(mask, fresh, stale[2, :, columns].astype(F32)).astype(BF16)
    for k in range(PARTS - 1):
        query_copy(k).wait_send()
        for h in range(HEADS_DEV):
            kv_copy(h, k).wait_send()
            out_copy(h, k).wait_send()


def step(
    tokens,
    projection_weight,
    shift_term,
    scale_term,
    query_gain,
    key_gain,
    stale_keys,
    stale_values,
    stale_output,
    refreshed,
):
    anywhere = pl.BlockSpec(memory_space=pl.ANY)
    vmem = pl.BlockSpec(memory_space=pltpu.VMEM)
    dma = pltpu.SemaphoreType.DMA
    others = PARTS - 1
    scratch = [
        pltpu.VMEM((ROWS, D), BF16),
        pltpu.VMEM((3, D, D), BF16),
        pltpu.VMEM((3, ROWS, D), BF16),
        pltpu.VMEM((ROWS, D), BF16),
        pltpu.VMEM((D, ROWS), BF16),
        pltpu.VMEM((ROWS, 128), F32),
        pltpu.VMEM((PARTS, HEADS_DEV, HD, ROWS), BF16),
        pltpu.VMEM((HEADS_DEV, PARTS, 2, HD, ROWS), BF16),
        pltpu.VMEM((PARTS, HEADS_DEV, HD, ROWS), BF16),
        pltpu.VMEM((HEADS_DEV, PARTS, 2, HD, ROWS), BF16),
        pltpu.VMEM((HEADS_DEV, TILES, TILE, HD), BF16),
        pltpu.VMEM((HEADS_DEV, REFRESHED, TILE, HD), BF16),
        pltpu.VMEM((HEADS_DEV, FRESH, HD), F32),
        pltpu.VMEM((HEADS_DEV, FRESH, 128), F32),
        pltpu.VMEM((HEADS_DEV, REFRESHED, TILE, HD), BF16),
        pltpu.VMEM((HEADS_DEV, PARTS, HD, ROWS), BF16),
        pltpu.VMEM((PARTS, HEADS_DEV, HD, ROWS), BF16),
        pltpu.VMEM((2, 256), jnp.int32),
        pltpu.SMEM((2, 256), jnp.int32),
        dma((TOKEN_LOADS,)),
        dma((3,)),
        dma((3,)),
        dma,
        dma((5,)),
        dma((others,)),
        dma((others,)),
        dma((HEADS_DEV, others)),
        dma((HEADS_DEV, others)),
        dma((HEADS_DEV, others)),
        dma((HEADS_DEV, others)),
    ]
    return pl.pallas_call(
        kernel,
        out_shape=jax.ShapeDtypeStruct((ROWS, D), BF16),
        in_specs=[anywhere, anywhere, vmem, vmem, vmem, vmem, anywhere, anywhere, anywhere, vmem],
        out_specs=vmem,
        scratch_shapes=scratch,
        compiler_params=pltpu.CompilerParams(
            collective_id=0, has_side_effects=True, vmem_limit_bytes=60 * 2**20
        ),
    )(
        tokens,
        projection_weight,
        shift_term,
        scale_term,
        query_gain,
        key_gain,
        stale_keys,
        stale_values,
        stale_output,
        refreshed,
    )


def solution(mesh):
    rows = P(("grp", "patch"), None)
    in_specs = (rows, P(), P(), P(), P(), P(), rows, rows, rows, P("grp"))
    return jax.shard_map(step, mesh=mesh, in_specs=in_specs, out_specs=rows, check_vma=False)
```

profile of v0, /device:TPU:32, one launch (start us, length us, event | category | flops | bytes accessed | tf_op | source)
XLA Modules:
  0.0 58.1 jit_solution(13237698392209253370)
XLA Ops:
  0.0 55.9 %shard_map.100 = bf16[384,1152]{1,0:T(8,128)(2,1)} custom-call(bf16[384,1152]{1,0:T(8,128)(2,1)} %tokens_hbm.1, bf16[1152,3456]{1,0:T(8,128)(2,1)} %weight_hbm.1, f32[1152]{0:T(1024)} %shift_ref.1, f32[1152]{0:T(1024)} %scale_ref.1, f32[72]{0:T(128)} %query_gain_ref.1, f32[72]{0:T(128)} %key_gain_ref.1, bf16[384,1152]{1,0:T(8,128)(2,1)} %stale_keys_hbm.1, ...), custom_call_target="tpu_custom_call" | custom-call | tf_op jit(solution)/shard_map/pallas_call | solution.py:398
  55.9 2.1 %copy.12 = bf16[384,1152]{1,0:T(8,128)(2,1)} copy(bf16[384,1152]{1,0:T(8,128)(2,1)} %shard_map.100) | data formatting | bytes 1769472
where the time goes:
time: 58.2 us; the launch traced here: 58.1 us
  Pallas kernels  55.9 us (96%)
  local copies, waits for them, and re-layouts  2.15 us (4%)
    pallas_call x1, Pallas kernels, step(): pl.pallas_call(kernel, out_shape=jax.ShapeDtypeStruct((ROWS, D), BF16), i...  55.9 us
    unnamed x1, local copies, waits for them, and re-layouts  2.15 us

commit v1 on v0

--- a/solution.py
+++ b/solution.py
@@ -21,8 +21,9 @@
 HEADS_DEV = H // PARTS
 BLOCK = 384
 QBLOCK = 256
-TOKEN_LOADS = 3
-NORM_BLOCK = 64
+QUERY_PARTS = 3
+QUERY_ROWS = ROWS // QUERY_PARTS
+NORM_BLOCK = 32
 MESH = pl.DeviceIdType.MESH
 EPSILON = 1e-06
 F32 = jnp.float32
@@ -48,15 +49,20 @@
 def kernel(
     tokens_hbm,
     weight_hbm,
+    shift_hbm,
+    scale_hbm,
+    query_gain_hbm,
+    key_gain_hbm,
+    stale_keys_hbm,
+    stale_values_hbm,
+    stale_output_hbm,
+    refreshed_hbm,
+    out_ref,
     shift_ref,
     scale_ref,
     query_gain_ref,
     key_gain_ref,
-    stale_keys_hbm,
-    stale_values_hbm,
-    stale_output_hbm,
     refreshed_ref,
-    out_ref,
     tokens,
     weight,
     stale,
@@ -76,6 +82,7 @@
     out_recv,
     plan_vmem,
     plan,
+    small_sem,
     load_sem,
     weight_sem,
     stale_sem,
@@ -100,9 +107,23 @@
         dy, dx = OFFSETS[k]
         return lax.rem(my_y + 4 - dy, 4) * 2 + lax.rem(my_x + dx, 2)
 
+    barrier = pltpu.get_barrier_semaphore()
+    for k in range(PARTS - 1):
+        pl.semaphore_signal(barrier, inc=1, device_id=(grp, target(k)), device_id_type=MESH)
+
+    small = (
+        (shift_hbm, shift_ref),
+        (scale_hbm, scale_ref),
+        (query_gain_hbm, query_gain_ref),
+        (key_gain_hbm, key_gain_ref),
+        (refreshed_hbm, refreshed_ref),
+    )
+    small_loads = [
+        pltpu.make_async_copy(there, here, small_sem.at[at]) for at, (there, here) in enumerate(small)
+    ]
     loads = []
-    for part in range(TOKEN_LOADS):
-        rows = pl.ds(part * (ROWS // TOKEN_LOADS), ROWS // TOKEN_LOADS)
+    for part in range(QUERY_PARTS):
+        rows = pl.ds(part * (ROWS // QUERY_PARTS), ROWS // QUERY_PARTS)
         loads.append(pltpu.make_async_copy(tokens_hbm.at[rows], tokens.at[rows], load_sem.at[part]))
     weight_loads = []
     for part in range(3):
@@ -113,15 +134,16 @@
     stale_loads = []
     for slot, ref in enumerate((stale_keys_hbm, stale_values_hbm, stale_output_hbm)):
         stale_loads.append(pltpu.make_async_copy(ref, stale.at[slot], stale_sem.at[slot]))
-    for load in loads:
+    loads[0].start()
+    for load in small_loads[:3]:
+        load.start()
+    weight_loads[0].start()
+    for load in loads[1:] + small_loads[3:]:
         load.start()
     for part in range(3):
-        weight_loads[part].start()
+        if part > 0:
+            weight_loads[part].start()
         stale_loads[part].start()
-
-    barrier = pltpu.get_barrier_semaphore()
-    for k in range(PARTS - 1):
-        pl.semaphore_signal(barrier, inc=1, device_id=(grp, target(k)), device_id_type=MESH)
 
     def column(gain_ref):
         same = lax.broadcasted_iota(jnp.int32, (HD, HD), 0) == lax.broadcasted_iota(
@@ -130,51 +152,41 @@
         row = jnp.broadcast_to(gain_ref[...].reshape(1, HD), (HD, HD))
         return jnp.sum(jnp.where(same, row, 0.0), axis=1, keepdims=True)
 
+    for load in small_loads[:3]:
+        load.wait()
     shift = shift_ref[...].reshape(1, D)
     scale = 1.0 + scale_ref[...].reshape(1, D)
-    with jax.named_scope("norm"):
-        for part in range(TOKEN_LOADS):
-            loads[part].wait()
-            for block in range(ROWS // TOKEN_LOADS // NORM_BLOCK):
-                rows = pl.ds(part * (ROWS // TOKEN_LOADS) + block * NORM_BLOCK, NORM_BLOCK)
-                values = tokens[rows, :].astype(F32)
-                center = values - jnp.mean(values, axis=-1, keepdims=True)
-                spread = jnp.mean(center * center, axis=-1, keepdims=True)
-                normed = center * (1.0 / jnp.sqrt(spread + EPSILON))
-                hidden[rows, :] = (normed * scale + shift).astype(BF16)
+
+    def modulate(first, count):
+        for block in range(count // NORM_BLOCK):
+            rows = pl.ds(first + block * NORM_BLOCK, NORM_BLOCK)
+            values = tokens[rows, :].astype(F32)
+            center = values - jnp.mean(values, axis=-1, keepdims=True)
+            spread = jnp.mean(center * center, axis=-1, keepdims=True)
+            normed = center * (1.0 / jnp.sqrt(spread + EPSILON))
+            hidden[rows, :] = (normed * scale + shift).astype(BF16)
 
     def project(part):
         for block in range(D // BLOCK):
             columns = pl.ds(block * BLOCK, BLOCK)
             fresh = dot(hidden[...], weight[part, :, columns]).astype(BF16)
-            if part > 0:
-                mask = own_mask[...]
-                mask = jnp.concatenate([mask] * (BLOCK // 128), axis=1)
-                old = stale[part - 1, :, columns].astype(F32)
-                fresh = jnp.where(mask > 0.5, fresh.astype(F32), old).astype(BF16)
+            mask = own_mask[...]
+            mask = jnp.concatenate([mask] * (BLOCK // 128), axis=1)
+            old = stale[part - 1, :, columns].astype(F32)
+            fresh = jnp.where(mask > 0.5, fresh.astype(F32), old).astype(BF16)
             turned[columns, :] = fresh.T
 
-    def head_norm(head, gain):
-        values = turned[pl.ds(head * HD, HD), :].astype(F32)
+    def head_norm(values, gain):
+        values = values.astype(F32)
         mean = jnp.sum(values * values, axis=0, keepdims=True) * (1.0 / HD)
         return (values * (1.0 / jnp.sqrt(mean + EPSILON)) * gain).astype(BF16)
 
-    with jax.named_scope("proj_q"):
-        weight_loads[0].wait()
-        project(0)
-    with jax.named_scope("norm_q"):
-        gain = column(query_gain_ref)
-        for head in range(H):
-            query_send[head // HEADS_DEV, head % HEADS_DEV] = head_norm(head, gain)
-    with jax.named_scope("barrier"):
-        pl.semaphore_wait(barrier, PARTS - 1)
-
-    def query_copy(k):
+    def query_copy(part, k):
         return pltpu.make_async_remote_copy(
-            src_ref=query_send.at[target(k)],
-            dst_ref=query_recv.at[me],
-            send_sem=q_send_sem.at[k],
-            recv_sem=q_recv_sem.at[k],
+            src_ref=query_send.at[part, target(k)],
+            dst_ref=query_recv.at[part, me],
+            send_sem=q_send_sem.at[part, k],
+            recv_sem=q_recv_sem.at[part, k],
             device_id=(grp, target(k)),
             device_id_type=MESH,
         )
@@ -199,19 +211,37 @@
             device_id_type=MESH,
         )
 
-    own_query = pltpu.make_async_copy(query_send.at[me], query_recv.at[me], own_sem.at[0])
-    own_kv = [
-        pltpu.make_async_copy(kv_send.at[h, me], kv_recv.at[h, me], own_sem.at[1 + h])
+    own_out = [
+        pltpu.make_async_copy(out_send.at[h, me], out_recv.at[me, h], own_sem.at[h])
         for h in range(HEADS_DEV)
     ]
-    own_out = [
-        pltpu.make_async_copy(out_send.at[h, me], out_recv.at[me, h], own_sem.at[3 + h])
-        for h in range(HEADS_DEV)
-    ]
-    for k in range(PARTS - 1):
-        query_copy(k).start()
-    own_query.start()
-
+
+    gain = column(query_gain_ref)
+    for part in range(QUERY_PARTS):
+        with jax.named_scope("norm"):
+            loads[part].wait()
+            modulate(part * QUERY_ROWS, QUERY_ROWS)
+        with jax.named_scope("proj_q"):
+            if part == 0:
+                weight_loads[0].wait()
+            rows = pl.ds(part * QUERY_ROWS, QUERY_ROWS)
+            for block in range(D // BLOCK):
+                columns = pl.ds(block * BLOCK, BLOCK)
+                fresh = dot(hidden[rows, :], weight[0, :, columns]).astype(BF16)
+                turned[columns, rows] = fresh.T
+        with jax.named_scope("norm_q"):
+            for head in range(H):
+                query_send[part, head // HEADS_DEV, head % HEADS_DEV] = head_norm(
+                    turned[pl.ds(head * HD, HD), rows], gain
+                )
+        if part == 0:
+            with jax.named_scope("barrier"):
+                pl.semaphore_wait(barrier, PARTS - 1)
+        for k in range(PARTS - 1):
+            query_copy(part, k).start()
+
+    for load in small_loads[3:]:
+        load.wait()
     flags = refreshed_ref[...].reshape(1, TILES).astype(F32)
     tile_row = lax.broadcasted_iota(jnp.int32, (TILES, TILES), 0)
     tile_col = lax.broadcasted_iota(jnp.int32, (TILES, TILES), 1)
@@ -240,7 +270,8 @@
     with jax.named_scope("norm_k"):
         gain = column(key_gain_ref)
         for head in range(H):
-            kv_send[head % HEADS_DEV, head // HEADS_DEV, 0] = head_norm(head, gain)
+            values = turned[pl.ds(head * HD, HD), :]
+            kv_send[head % HEADS_DEV, head // HEADS_DEV, 0] = head_norm(values, gain)
     with jax.named_scope("proj_v"):
         weight_loads[2].wait()
         stale_loads[1].wait()
@@ -251,23 +282,26 @@
     for h in range(HEADS_DEV):
         for k in range(PARTS - 1):
             kv_copy(h, k).start()
-        own_kv[h].start()
 
     numerator[...] = jnp.zeros_like(numerator)
     totals[...] = jnp.zeros_like(totals)
-    same = eye(ROWS)
-
-    def turn_queries(index):
+    same = eye(QUERY_ROWS)
+    part_tiles = QUERY_ROWS // TILE
+
+    def turn_queries(buffer, part, index):
         for h in range(HEADS_DEV):
-            rows = dot_nt(same, query_recv[index, h]).astype(BF16)
-            query_rows[h, pl.ds(index * TILES_DEV, TILES_DEV)] = rows.reshape(TILES_DEV, TILE, HD)
+            rows = dot_nt(same, buffer[part, index, h]).astype(BF16)
+            tiles = pl.ds(index * TILES_DEV + part * part_tiles, part_tiles)
+            query_rows[h, tiles] = rows.reshape(part_tiles, TILE, HD)
 
     with jax.named_scope("turn_q"):
-        own_query.wait()
-        turn_queries(me)
-        for k in range(PARTS - 1):
-            query_copy(k).wait_recv()
-            turn_queries(source(k))
+        for part in range(QUERY_PARTS):
+            turn_queries(query_send, part, me)
+        for part in range(QUERY_PARTS):
+            for k in range(PARTS - 1):
+                with jax.named_scope(f"wait_q#p={part}#k={k}"):
+                    query_copy(part, k).wait_recv()
+                turn_queries(query_recv, part, source(k))
     with jax.named_scope("keep_fresh"):
         plan_copy.wait()
         for slot in range(REFRESHED):
@@ -277,17 +311,16 @@
     factor = math.log2(math.e) / math.sqrt(HD)
     tiles_block = QBLOCK // TILE
 
-    def add_block(head, index):
-        keys = kv_recv[head, index, 0]
-        values = kv_recv[head, index, 1]
-
+    def add_blocks(head, blocks):
+        keys = jnp.concatenate([ref[head, index, 0] for ref, index in blocks], axis=1)
+        values = jnp.concatenate([ref[head, index, 1] for ref, index in blocks], axis=1)
         for block in range(FRESH // QBLOCK):
             rows = pl.ds(block * QBLOCK, QBLOCK)
             queries = query_fresh[head, pl.ds(block * tiles_block, tiles_block)]
             scores = dot(queries.reshape(QBLOCK, HD), keys)
             weights = jnp.exp2(scores * factor)
             sums = weights[:, 0:128]
-            for lane in range(128, ROWS, 128):
+            for lane in range(128, ROWS * len(blocks), 128):
                 sums = sums + weights[:, lane : lane + 128]
             totals[head, rows, :] += sums
             numerator[head, rows, :] += dot_nt(weights.astype(BF16), values)
@@ -314,14 +347,15 @@
         own_out[head].start()
 
     for h in range(HEADS_DEV):
-        with jax.named_scope("add_own"):
-            own_kv[h].wait()
-            add_block(h, me)
-        for k in range(PARTS - 1):
-            with jax.named_scope(f"wait_kv#h={h}#k={k}"):
-                kv_copy(h, k).wait_recv()
+        for step in ((0,), (1, 2), (3, 4), (5, 6)):
+            with jax.named_scope(f"wait_kv#h={h}#k={step[0]}"):
+                for k in step:
+                    kv_copy(h, k).wait_recv()
             with jax.named_scope("add"):
-                add_block(h, source(k))
+                blocks = [(kv_recv, source(k)) for k in step]
+                if len(step) == 1:
+                    blocks.append((kv_send, me))
+                add_blocks(h, blocks)
         with jax.named_scope("send_out"):
             send_out(h)
 
@@ -341,7 +375,8 @@
             fresh = turned[columns, :].T.astype(F32)
             out_ref[:, columns] = jnp.where(mask, fresh, stale[2, :, columns].astype(F32)).astype(BF16)
     for k in range(PARTS - 1):
-        query_copy(k).wait_send()
+        for part in range(QUERY_PARTS):
+            query_copy(part, k).wait_send()
         for h in range(HEADS_DEV):
             kv_copy(h, k).wait_send()
             out_copy(h, k).wait_send()
@@ -359,20 +394,25 @@
     stale_output,
     refreshed,
 ):
-    anywhere = pl.BlockSpec(memory_space=pl.ANY)
+    hbm = pl.BlockSpec(memory_space=pltpu.HBM)
     vmem = pl.BlockSpec(memory_space=pltpu.VMEM)
     dma = pltpu.SemaphoreType.DMA
     others = PARTS - 1
     scratch = [
+        pltpu.VMEM((D,), F32),
+        pltpu.VMEM((D,), F32),
+        pltpu.VMEM((HD,), F32),
+        pltpu.VMEM((HD,), F32),
+        pltpu.VMEM((TILES,), jnp.int32),
         pltpu.VMEM((ROWS, D), BF16),
         pltpu.VMEM((3, D, D), BF16),
         pltpu.VMEM((3, ROWS, D), BF16),
         pltpu.VMEM((ROWS, D), BF16),
         pltpu.VMEM((D, ROWS), BF16),
         pltpu.VMEM((ROWS, 128), F32),
-        pltpu.VMEM((PARTS, HEADS_DEV, HD, ROWS), BF16),
+        pltpu.VMEM((QUERY_PARTS, PARTS, HEADS_DEV, HD, QUERY_ROWS), BF16),
         pltpu.VMEM((HEADS_DEV, PARTS, 2, HD, ROWS), BF16),
-        pltpu.VMEM((PARTS, HEADS_DEV, HD, ROWS), BF16),
+        pltpu.VMEM((QUERY_PARTS, PARTS, HEADS_DEV, HD, QUERY_ROWS), BF16),
         pltpu.VMEM((HEADS_DEV, PARTS, 2, HD, ROWS), BF16),
         pltpu.VMEM((HEADS_DEV, TILES, TILE, HD), BF16),
         pltpu.VMEM((HEADS_DEV, REFRESHED, TILE, HD), BF16),
@@ -383,13 +423,14 @@
         pltpu.VMEM((PARTS, HEADS_DEV, HD, ROWS), BF16),
         pltpu.VMEM((2, 256), jnp.int32),
         pltpu.SMEM((2, 256), jnp.int32),
-        dma((TOKEN_LOADS,)),
+        dma((5,)),
+        dma((QUERY_PARTS,)),
         dma((3,)),
         dma((3,)),
         dma,
-        dma((5,)),
-        dma((others,)),
-        dma((others,)),
+        dma((HEADS_DEV,)),
+        dma((QUERY_PARTS, others)),
+        dma((QUERY_PARTS, others)),
         dma((HEADS_DEV, others)),
         dma((HEADS_DEV, others)),
         dma((HEADS_DEV, others)),
@@ -398,11 +439,11 @@
     return pl.pallas_call(
         kernel,
         out_shape=jax.ShapeDtypeStruct((ROWS, D), BF16),
-        in_specs=[anywhere, anywhere, vmem, vmem, vmem, vmem, anywhere, anywhere, anywhere, vmem],
+        in_specs=[hbm] * 10,
         out_specs=vmem,
         scratch_shapes=scratch,
         compiler_params=pltpu.CompilerParams(
-            collective_id=0, has_side_effects=True, vmem_limit_bytes=60 * 2**20
+            collective_id=0, has_side_effects=True, vmem_limit_bytes=63 * 2**20
         ),
     )(
         tokens,

time: 58.2 us -> 50.9 us (0.87)
  Pallas kernels: 55.9 us -> 48.6 us
    pallas_call x1, Pallas kernels: 55.9 us -> 48.6 us  [step(): pl.pallas_call(kernel, out_shape=jax.ShapeDtypeStruct((ROWS, D), BF16), i...]
where the time goes in v1:
time: 50.9 us; the launch traced here: 50.8 us
  Pallas kernels  48.6 us (95%)
  local copies, waits for them, and re-layouts  2.15 us (4%)
    pallas_call x1, Pallas kernels, step(): pl.pallas_call(kernel, out_shape=jax.ShapeDtypeStruct((ROWS, D), BF16), i...  48.6 us
    unnamed x1, local copies, waits for them, and re-layouts  2.15 us

profile of v1, /device:TPU:32, one launch (start us, length us, event | category | flops | bytes accessed | tf_op | source)
XLA Modules:
  0.0 50.8 jit_solution(13672762281147803334)
XLA Ops:
  0.0 48.6 %shard_map.100 = bf16[384,1152]{1,0:T(8,128)(2,1)} custom-call(bf16[384,1152]{1,0:T(8,128)(2,1)} %tokens_hbm.1, bf16[1152,3456]{1,0:T(8,128)(2,1)} %weight_hbm.1, f32[1152]{0:T(1024)} %shift_hbm.1, f32[1152]{0:T(1024)} %scale_hbm.1, f32[72]{0:T(128)} %query_gain_hbm.1, f32[72]{0:T(128)} %key_gain_hbm.1, bf16[384,1152]{1,0:T(8,128)(2,1)} %stale_keys_hbm.1, ...), custom_call_target="tpu_custom_call" | custom-call | tf_op jit(solution)/shard_map/pallas_call | solution.py:439
  48.7 2.1 %copy.12 = bf16[384,1152]{1,0:T(8,128)(2,1)} copy(bf16[384,1152]{1,0:T(8,128)(2,1)} %shard_map.100) | data formatting | bytes 1769472

commit v2 on v1

--- a/solution.py
+++ b/solution.py
@@ -22,6 +22,16 @@
 BLOCK = 384
 QBLOCK = 256
 QUERY_PARTS = 3
+STEPS = (
+    (0, (0,)),
+    (0, (1, 2)),
+    (0, (3, 4)),
+    (1, (0,)),
+    (0, (5, 6)),
+    (1, (1, 2)),
+    (1, (3, 4)),
+    (1, (5, 6)),
+)
 QUERY_ROWS = ROWS // QUERY_PARTS
 NORM_BLOCK = 32
 MESH = pl.DeviceIdType.MESH
@@ -30,6 +40,8 @@
 BF16 = jnp.bfloat16
 
 OFFSETS = ((2, 1), (2, 0), (1, 1), (3, 1), (0, 1), (1, 0), (3, 0))
+
+STEP_OF = (0, 1, 1, 2, 2, 3, 3)
 
 
 def dot(a, b):
@@ -57,7 +69,7 @@
     stale_values_hbm,
     stale_output_hbm,
     refreshed_hbm,
-    out_ref,
+    out_hbm,
     shift_ref,
     scale_ref,
     query_gain_ref,
@@ -80,6 +92,7 @@
     attended,
     out_send,
     out_recv,
+    result,
     plan_vmem,
     plan,
     small_sem,
@@ -87,6 +100,7 @@
     weight_sem,
     stale_sem,
     plan_sem,
+    store_sem,
     own_sem,
     q_send_sem,
     q_recv_sem,
@@ -185,8 +199,8 @@
         return pltpu.make_async_remote_copy(
             src_ref=query_send.at[part, target(k)],
             dst_ref=query_recv.at[part, me],
-            send_sem=q_send_sem.at[part, k],
-            recv_sem=q_recv_sem.at[part, k],
+            send_sem=q_send_sem,
+            recv_sem=q_recv_sem.at[k],
             device_id=(grp, target(k)),
             device_id_type=MESH,
         )
@@ -195,8 +209,8 @@
         return pltpu.make_async_remote_copy(
             src_ref=kv_send.at[head, target(k)],
             dst_ref=kv_recv.at[head, me],
-            send_sem=kv_send_sem.at[head, k],
-            recv_sem=kv_recv_sem.at[head, k],
+            send_sem=kv_send_sem,
+            recv_sem=kv_recv_sem.at[head, STEP_OF[k]],
             device_id=(grp, target(k)),
             device_id_type=MESH,
         )
@@ -205,16 +219,17 @@
         return pltpu.make_async_remote_copy(
             src_ref=out_send.at[head, target(k)],
             dst_ref=out_recv.at[me, head],
-            send_sem=o_send_sem.at[head, k],
-            recv_sem=o_recv_sem.at[head, k],
+            send_sem=o_send_sem,
+            recv_sem=o_recv_sem,
             device_id=(grp, target(k)),
             device_id_type=MESH,
         )
 
-    own_out = [
-        pltpu.make_async_copy(out_send.at[h, me], out_recv.at[me, h], own_sem.at[h])
-        for h in range(HEADS_DEV)
-    ]
+    def own_out(head):
+        return pltpu.make_async_copy(out_send.at[head, me], out_recv.at[me, head], own_sem)
+
+    def wait_bytes(ref, sem):
+        pltpu.make_async_copy(ref, ref, sem).wait()
 
     gain = column(query_gain_ref)
     for part in range(QUERY_PARTS):
@@ -297,10 +312,10 @@
     with jax.named_scope("turn_q"):
         for part in range(QUERY_PARTS):
             turn_queries(query_send, part, me)
-        for part in range(QUERY_PARTS):
-            for k in range(PARTS - 1):
-                with jax.named_scope(f"wait_q#p={part}#k={k}"):
-                    query_copy(part, k).wait_recv()
+        for k in range(PARTS - 1):
+            with jax.named_scope(f"wait_q#k={k}"):
+                wait_bytes(query_recv.at[:, source(k)], q_recv_sem.at[k])
+            for part in range(QUERY_PARTS):
                 turn_queries(query_recv, part, source(k))
     with jax.named_scope("keep_fresh"):
         plan_copy.wait()
@@ -344,42 +359,45 @@
             out_send[head, owner] = dot_nt(same, rows).astype(BF16)
         for k in range(PARTS - 1):
             out_copy(head, k).start()
-        own_out[head].start()
-
-    for h in range(HEADS_DEV):
-        for step in ((0,), (1, 2), (3, 4), (5, 6)):
-            with jax.named_scope(f"wait_kv#h={h}#k={step[0]}"):
-                for k in step:
-                    kv_copy(h, k).wait_recv()
-            with jax.named_scope("add"):
-                blocks = [(kv_recv, source(k)) for k in step]
-                if len(step) == 1:
-                    blocks.append((kv_send, me))
-                add_blocks(h, blocks)
-        with jax.named_scope("send_out"):
-            send_out(h)
+        own_out(head).start()
+
+    for h, step in STEPS:
+        with jax.named_scope(f"wait_kv#h={h}#k={step[0]}"):
+            wait_bytes(kv_recv.at[h, pl.ds(0, len(step))], kv_recv_sem.at[h, STEP_OF[step[0]]])
+        with jax.named_scope("add"):
+            blocks = [(kv_recv, source(k)) for k in step]
+            if len(step) == 1:
+                blocks.append((kv_send, me))
+            add_blocks(h, blocks)
+        if step == STEPS[-1][1]:
+            with jax.named_scope("send_out"):
+                send_out(h)
 
     with jax.named_scope("wait_out"):
         stale_loads[2].wait()
-        for h in range(HEADS_DEV):
-            own_out[h].wait()
-            for k in range(PARTS - 1):
-                out_copy(h, k).wait_recv()
+        wait_bytes(out_recv.at[me], own_sem)
+        wait_bytes(out_recv.at[pl.ds(0, PARTS - 1)], o_recv_sem)
     with jax.named_scope("merge"):
-        for owner in range(PARTS):
-            for h in range(HEADS_DEV):
-                turned[pl.ds((owner * HEADS_DEV + h) * HD, HD), :] = out_recv[owner, h]
         mask = own_mask[...] > 0.5
         for block in range(D // 128):
             columns = pl.ds(block * 128, 128)
+            heads = range(block * 128 // HD, (block * 128 + 127) // HD + 1)
+            for head in heads:
+                if head * HD >= block * 128 or block == 0:
+                    turned[pl.ds(head * HD, HD), :] = out_recv[head // HEADS_DEV, head % HEADS_DEV]
             fresh = turned[columns, :].T.astype(F32)
-            out_ref[:, columns] = jnp.where(mask, fresh, stale[2, :, columns].astype(F32)).astype(BF16)
-    for k in range(PARTS - 1):
-        for part in range(QUERY_PARTS):
-            query_copy(part, k).wait_send()
-        for h in range(HEADS_DEV):
-            kv_copy(h, k).wait_send()
-            out_copy(h, k).wait_send()
+            old = stale[2, :, columns].astype(F32)
+            result[:, columns] = jnp.where(mask, fresh, old).astype(BF16)
+            if block % 3 == 2:
+                columns = pl.ds((block - 2) * 128, 3 * 128)
+                pltpu.make_async_copy(
+                    result.at[:, columns], out_hbm.at[:, columns], store_sem
+                ).start()
+    with jax.named_scope("wait_end"):
+        wait_bytes(query_send.at[:, pl.ds(0, PARTS - 1)], q_send_sem)
+        wait_bytes(kv_send.at[:, pl.ds(0, PARTS - 1)], kv_send_sem)
+        wait_bytes(out_send.at[:, pl.ds(0, PARTS - 1)], o_send_sem)
+        pltpu.make_async_copy(result, out_hbm, store_sem).wait()
 
 
 def step(
@@ -395,7 +413,6 @@
     refreshed,
 ):
     hbm = pl.BlockSpec(memory_space=pltpu.HBM)
-    vmem = pl.BlockSpec(memory_space=pltpu.VMEM)
     dma = pltpu.SemaphoreType.DMA
     others = PARTS - 1
     scratch = [
@@ -421,6 +438,7 @@
         pltpu.VMEM((HEADS_DEV, REFRESHED, TILE, HD), BF16),
         pltpu.VMEM((HEADS_DEV, PARTS, HD, ROWS), BF16),
         pltpu.VMEM((PARTS, HEADS_DEV, HD, ROWS), BF16),
+        pltpu.VMEM((ROWS, D), BF16),
         pltpu.VMEM((2, 256), jnp.int32),
         pltpu.SMEM((2, 256), jnp.int32),
         dma((5,)),
@@ -428,19 +446,20 @@
         dma((3,)),
         dma((3,)),
         dma,
-        dma((HEADS_DEV,)),
-        dma((QUERY_PARTS, others)),
-        dma((QUERY_PARTS, others)),
-        dma((HEADS_DEV, others)),
-        dma((HEADS_DEV, others)),
-        dma((HEADS_DEV, others)),
-        dma((HEADS_DEV, others)),
+        dma,
+        dma,
+        dma,
+        dma((others,)),
+        dma,
+        dma((HEADS_DEV, 4)),
+        dma,
+        dma,
     ]
     return pl.pallas_call(
         kernel,
         out_shape=jax.ShapeDtypeStruct((ROWS, D), BF16),
         in_specs=[hbm] * 10,
-        out_specs=vmem,
+        out_specs=hbm,
         scratch_shapes=scratch,
         compiler_params=pltpu.CompilerParams(
             collective_id=0, has_side_effects=True, vmem_limit_bytes=63 * 2**20

time: 50.9 us -> 49.7 us (0.976)
  Pallas kernels: 48.6 us -> 47.4 us
    pallas_call x1, Pallas kernels: 48.6 us -> 47.4 us  [step(): pl.pallas_call(kernel, out_shape=jax.ShapeDtypeStruct((ROWS, D), BF16), i...]
where the time goes in v2:
time: 49.7 us; the launch traced here: 49.5 us
  Pallas kernels  47.4 us (95%)
  local copies, waits for them, and re-layouts  2.15 us (4%)
    pallas_call x1, Pallas kernels, step(): pl.pallas_call(kernel, out_shape=jax.ShapeDtypeStruct((ROWS, D), BF16), i...  47.4 us
    unnamed x1, local copies, waits for them, and re-layouts  2.15 us

profile of v2, /device:TPU:32, one launch (start us, length us, event | category | flops | bytes accessed | tf_op | source)
XLA Modules:
  0.0 49.5 jit_solution(5084277148852439319)
XLA Ops:
  0.0 47.4 %shard_map.100 = bf16[384,1152]{1,0:T(8,128)(2,1)} custom-call(bf16[384,1152]{1,0:T(8,128)(2,1)} %tokens_hbm.1, bf16[1152,3456]{1,0:T(8,128)(2,1)} %weight_hbm.1, f32[1152]{0:T(1024)} %shift_hbm.1, f32[1152]{0:T(1024)} %scale_hbm.1, f32[72]{0:T(128)} %query_gain_hbm.1, f32[72]{0:T(128)} %key_gain_hbm.1, bf16[384,1152]{1,0:T(8,128)(2,1)} %stale_keys_hbm.1, ...), custom_call_target="tpu_custom_call" | custom-call | tf_op jit(solution)/shard_map/pallas_call | solution.py:458
  47.4 2.1 %copy.12 = bf16[384,1152]{1,0:T(8,128)(2,1)} copy(bf16[384,1152]{1,0:T(8,128)(2,1)} %shard_map.100) | data formatting | bytes 1769472

commit v3 on v2

--- a/solution.py
+++ b/solution.py
@@ -350,15 +350,18 @@
             )
 
         same = eye(HD)
-        for owner in range(PARTS):
-            pieces = []
-            for tile in range(TILES_DEV):
-                item = jnp.clip(plan[1, owner * TILES_DEV + tile], 0, REFRESHED - 1)
-                pieces.append(attended[head, item])
-            rows = jnp.concatenate(pieces, axis=0)
-            out_send[head, owner] = dot_nt(same, rows).astype(BF16)
-        for k in range(PARTS - 1):
-            out_copy(head, k).start()
+        for group in ((0, 1, 2, 3), (4, 5, 6, 7)):
+            for k in group:
+                owner = target(k) if k < PARTS - 1 else me
+                pieces = []
+                for tile in range(TILES_DEV):
+                    item = jnp.clip(plan[1, owner * TILES_DEV + tile], 0, REFRESHED - 1)
+                    pieces.append(attended[head, item])
+                rows = jnp.concatenate(pieces, axis=0)
+                out_send[head, owner] = dot_nt(same, rows).astype(BF16)
+            for k in group:
+                if k < PARTS - 1:
+                    out_copy(head, k).start()
         own_out(head).start()
 
     for h, step in STEPS:

time: 49.7 us -> 49.6 us (level)
  no operation moved by 1% of the time
where the time goes in v3:
time: 49.6 us; the launch traced here: 49.5 us
  Pallas kernels  47.3 us (95%)
  local copies, waits for them, and re-layouts  2.15 us (4%)
    pallas_call x1, Pallas kernels, step(): pl.pallas_call(kernel, out_shape=jax.ShapeDtypeStruct((ROWS, D), BF16), i...  47.3 us
    unnamed x1, local copies, waits for them, and re-layouts  2.15 us

profile of v3, /device:TPU:32, one launch (start us, length us, event | category | flops | bytes accessed | tf_op | source)
XLA Modules:
  0.0 49.5 jit_solution(8707607852740616370)
XLA Ops:
  0.0 47.3 %shard_map.100 = bf16[384,1152]{1,0:T(8,128)(2,1)} custom-call(bf16[384,1152]{1,0:T(8,128)(2,1)} %tokens_hbm.1, bf16[1152,3456]{1,0:T(8,128)(2,1)} %weight_hbm.1, f32[1152]{0:T(1024)} %shift_hbm.1, f32[1152]{0:T(1024)} %scale_hbm.1, f32[72]{0:T(128)} %query_gain_hbm.1, f32[72]{0:T(128)} %key_gain_hbm.1, bf16[384,1152]{1,0:T(8,128)(2,1)} %stale_keys_hbm.1, ...), custom_call_target="tpu_custom_call" | custom-call | tf_op jit(solution)/shard_map/pallas_call | solution.py:461
  47.3 2.1 %copy.12 = bf16[384,1152]{1,0:T(8,128)(2,1)} copy(bf16[384,1152]{1,0:T(8,128)(2,1)} %shard_map.100) | data formatting | bytes 1769472
